TPU v7x, 128 devices: a whole 4x4x4 slice. The times are simulated.
128 devices in a mesh: row: 8 (over z, core), col: 16 (over y, x).
Axes of the slice: x: 4, y: 4, z: 4, core: 2. Of those that a mesh axis runs over, the one named last changes fastest.
Arguments:
- right_side: float32 [512, 4096], P('row', 'col'), may hold values from -20 to 20
- initial_guess: float32 [512, 4096], P('row', 'col'), may hold values from -3 to 3
- kernel: float32 [31, 31], replicated, may hold values from 0 to 1, as said below
Outputs:
- template: float32 [512, 4096], P('row', 'col')
- residual: float32 [512, 4096], P('row', 'col')
Inputs may be any that keep to these rules, and one draw needn't show every extreme that they name: `kernel`: entries are positive and sum to one.
All inputs are finite; a program needn't handle non-finite values.
Results may differ from a plain program's by a relative error of at most 0.0003.
Values sent between devices are 32-bit elements; how exact they have to be, the bound alone decides.
A program may use at most 128 MiB of HBM per device.

v0:
```python
import math
import jax
import jax.numpy as jnp
from jax import lax
from jax.sharding import Mesh
from jax.sharding import PartitionSpec as P

ITERS = 3
ROW_COL = ("row_0", "row_1", "col_0", "col_1")
ROW = ("row_0", "row_1")
COL = ("col_0", "col_1")
penalty = 0.05


def with_halo(x, sides, width):
    for axis, dim in sides:
        count, length = (lax.axis_size(axis), x.shape[dim])
        up = [(i, (i + 1) % count) for i in range(count - 1)]
        down = [(j, i) for i, j in up]
        last = lax.slice_in_dim(x, length - width, length, axis=dim)
        initial = lax.slice_in_dim(x, 0, width, axis=dim)
        before = lax.ppermute(last, axis, up)
        after = lax.ppermute(initial, axis, down)
        x = jnp.concatenate([before, x, after], axis=dim)
    return x


def one_axis_at_a_time(x, axes):
    for axis in axes:
        x = lax.psum(x, axis)
    return x


def banded_tables(taps, block_width):
    width = taps.shape[0]
    span = block_width + width - 1
    offset = (
        jnp.arange(span, dtype=jnp.int32)[:, None]
        - jnp.arange(block_width, dtype=jnp.int32)[None, :]
    )
    selector = (offset[None, :, :] == jnp.arange(width, dtype=jnp.int32)[:, None, None]).astype(
        jnp.float32
    )
    return jnp.einsum("ab,bkj->akj", taps, selector, precision=lax.Precision.HIGHEST)


def correlate(padded, taps):
    width = taps.shape[0]
    out_rows = padded.shape[0] - width + 1
    out_cols = padded.shape[1] - width + 1
    block_width = math.gcd(out_cols, 128)
    count = out_cols // block_width
    span = block_width + width - 1
    tables = banded_tables(taps, block_width)
    blocks = jnp.stack(
        [padded[:, index * block_width : index * block_width + span] for index in range(count)],
        axis=1,
    )
    total = jnp.zeros((out_rows, count, block_width), jnp.float32)
    for shift_row in range(width):
        window = blocks[shift_row : shift_row + out_rows]
        total = total + jnp.einsum(
            "rnk,kj->rnj", window, tables[shift_row], precision=lax.Precision.HIGHEST
        )
    return total.reshape(out_rows, out_cols)


def laplacian(padded, margin, tile_rows, tile_cols):
    center = padded[margin : margin + tile_rows, margin : margin + tile_cols]
    upper = padded[margin - 1 : margin - 1 + tile_rows, margin : margin + tile_cols]
    lower = padded[margin + 1 : margin + 1 + tile_rows, margin : margin + tile_cols]
    leftward = padded[margin : margin + tile_rows, margin - 1 : margin - 1 + tile_cols]
    rightward = padded[margin : margin + tile_rows, margin + 1 : margin + 1 + tile_cols]
    return 4.0 * center - upper - lower - leftward - rightward


def operate(source, kernel):
    tile_rows, tile_cols = source.shape
    half_width = kernel.shape[0] // 2
    flipped = kernel[::-1, ::-1]
    padded = with_halo(source, ((ROW, 0), (COL, 1)), half_width)
    blurred = correlate(padded, kernel)
    blurred_pad = with_halo(blurred, ((ROW, 0), (COL, 1)), half_width)
    back = correlate(blurred_pad, flipped)
    smooth_term = laplacian(padded, half_width, tile_rows, tile_cols)
    return back + penalty * smooth_term


def paired(residual, applied):
    return (
        one_axis_at_a_time(jnp.sum(residual * residual), ROW_COL),
        one_axis_at_a_time(jnp.sum(residual * applied), ROW_COL),
    )


def on_device(right_side, initial_guess, kernel):
    template = initial_guess
    residual = right_side - operate(template, kernel)
    applied = operate(residual, kernel)
    norm_now, product = paired(residual, applied)
    step_size = norm_now / product
    direction, along = (residual, applied)
    for iteration in range(ITERS):
        template = template + step_size * direction
        residual = residual - step_size * along
        if iteration + 1 < ITERS:
            applied = operate(residual, kernel)
            norm_next, product = paired(residual, applied)
            ratio = norm_next / norm_now
            step_size = norm_next / (product - ratio * norm_next / step_size)
            direction = residual + ratio * direction
            along = applied + ratio * along
            norm_now = norm_next
    return (template, residual)


def solution(mesh):
    torus = Mesh(mesh.devices.reshape(4, 2, 4, 4), ("row_0", "row_1", "col_0", "col_1"))
    placed = (P(ROW, COL), P(ROW, COL), P())
    return jax.shard_map(
        on_device,
        mesh=torus,
        in_specs=placed,
        out_specs=(P(ROW, COL), P(ROW, COL)),
        check_vma=False,
    )
```

profile of v0, /device:TPU:2, one launch (start us, length us, event | category | flops | bytes accessed | tf_op | source)
XLA Modules:
  0.0 353.5 jit_solution(8451478255131608723)
XLA Ops:
  1.4 1.7 collective-permute-start
  3.1 1.3 collective-permute-start.1
  5.2 2.0 fusion.2
  7.3 1.3 fusion.3
  8.6 1.3 fusion.1273
  10.0 1.3 fusion.1275
  11.4 1.9 collective-permute-start.3
  13.4 4.1 %collective-permute-start.2 = (f32[94,15]{1,0:T(8,128)S(1)}, f32[94,15]{1,0:T(8,128)S(1)}, u32[]{:S(2)}, u32[]{:S(2)}) collective-permute-start(f32[94,15]{1,0:T(8,128)S(1)} %get-tuple-element.128), channel_id=1, source_target_pairs={{0,1},{1,2},{2,3},{3,4},{4,5},{5,6},{6,7},{7,8},{8,9},{9,10},{10,1... | collective-permute-start | bytes 16928 | tf_op jit(solution)/shard_map/ppermute | solution.py:22
  28.0 1.3 collective-permute-start.5
  29.3 4.4 %collective-permute-start.4 = (f32[15,256]{1,0:T(8,128)S(1)}, f32[15,256]{1,0:T(8,128)S(1)}, u32[]{:S(2)}, u32[]{:S(2)}) collective-permute-start(f32[15,256]{1,0:T(8,128)S(1)} %bitcast.674), channel_id=1, source_target_pairs={{0,16},{16,32},{32,48},{48,64},{64,80},{80,96},{96,112},{1,17},{17... | collective-permute-start | bytes 46088 | tf_op jit(solution)/shard_map/ppermute | solution.py:22
  34.7 1.9 collective-permute-start.7
  36.6 4.1 %collective-permute-start.6 = (f32[94,15]{1,0:T(8,128)S(1)}, f32[94,15]{1,0:T(8,128)S(1)}, u32[]{:S(2)}, u32[]{:S(2)}) collective-permute-start(f32[94,15]{1,0:T(8,128)S(1)} %get-tuple-element.124), channel_id=1, source_target_pairs={{0,1},{1,2},{2,3},{3,4},{4,5},{5,6},{6,7},{7,8},{8,9},{9,10},{10,1... | collective-permute-start | bytes 16928 | tf_op jit(solution)/shard_map/ppermute | solution.py:22
  51.3 3.9 %collective-permute-start.8 = (f32[15,256]{1,0:T(8,128)S(1)}, f32[15,256]{1,0:T(8,128)S(1)}, u32[]{:S(2)}, u32[]{:S(2)}) collective-permute-start(f32[15,256]{1,0:T(8,128)S(1)} %get-tuple-element.141), channel_id=1, source_target_pairs={{0,16},{16,32},{32,48},{48,64},{64,80},{80,96},{96,112},{1,17},{17... | collective-permute-start | bytes 46088 | tf_op jit(solution)/shard_map/ppermute | solution.py:22
  55.2 1.3 collective-permute-start.9
  56.5 4.7 %collective-permute-done.9 = f32[15,256]{1,0:T(8,128)S(1)} collective-permute-done((f32[15,256]{1,0:T(8,128)S(1)}, f32[15,256]{1,0:T(8,128)S(1)}, u32[]{:S(2)}, u32[]{:S(2)}) %collective-permute-start.9) | collective-permute-done | bytes 15392 | tf_op jit(solution)/shard_map/ppermute | solution.py:23
  61.3 3.9 %collective-permute-start.10 = (f32[94,15]{1,0:T(8,128)S(1)}, f32[94,15]{1,0:T(8,128)S(1)}, u32[]{:S(2)}, u32[]{:S(2)}) collective-permute-start(f32[94,15]{1,0:T(8,128)S(1)} %get-tuple-element.119), channel_id=1, source_target_pairs={{0,1},{1,2},{2,3},{3,4},{4,5},{5,6},{6,7},{7,8},{8,9},{9,10},{10,1... | collective-permute-start | bytes 16928 | tf_op jit(solution)/shard_map/ppermute | solution.py:22
  65.3 2.2 collective-permute-start.11
  67.5 5.8 %collective-permute-done.11 = f32[94,15]{1,0:T(8,128)S(1)} collective-permute-done((f32[94,15]{1,0:T(8,128)S(1)}, f32[94,15]{1,0:T(8,128)S(1)}, u32[]{:S(2)}, u32[]{:S(2)}) %collective-permute-start.11) | collective-permute-done | bytes 5672 | tf_op jit(solution)/shard_map/ppermute | solution.py:23
  82.1 1.3 collective-permute-start.13
  83.4 3.8 %collective-permute-start.12 = (f32[15,256]{1,0:T(8,128)S(1)}, f32[15,256]{1,0:T(8,128)S(1)}, u32[]{:S(2)}, u32[]{:S(2)}) collective-permute-start(f32[15,256]{1,0:T(8,128)S(1)} %bitcast.675), channel_id=1, source_target_pairs={{0,16},{16,32},{32,48},{48,64},{64,80},{80,96},{96,112},{1,17},{17... | collective-permute-start | bytes 46088 | tf_op jit(solution)/shard_map/ppermute | solution.py:22
  88.1 1.9 collective-permute-start.15
  90.1 6.7 %collective-permute-start.14 = (f32[94,15]{1,0:T(8,128)S(1)}, f32[94,15]{1,0:T(8,128)S(1)}, u32[]{:S(2)}, u32[]{:S(2)}) collective-permute-start(f32[94,15]{1,0:T(8,128)S(1)} %get-tuple-element.116), channel_id=1, source_target_pairs={{0,1},{1,2},{2,3},{3,4},{4,5},{5,6},{6,7},{7,8},{8,9},{9,10},{10,1... | collective-permute-start | bytes 16928 | tf_op jit(solution)/shard_map/ppermute | solution.py:22
  96.8 1.4 collective-permute-done.14
  107.6 14.4 %all-reduce.8 = (f32[]{:T(128)}, f32[]{:T(128)}) all-reduce(f32[]{:T(128)} %get-tuple-element.7, f32[]{:T(128)} %get-tuple-element.6), channel_id=1, replica_groups=mesh['row_0'=4,'row_1'=2,'col_0'=4,'col_1'=4] {'row_0'}, use_global_device_ids=true, to_apply=%region_1.0 | all-reduce | flops 2 | bytes 16 | tf_op jit(solution)/shard_map/psum | solution.py:30
  122.0 3.1 all-reduce.11
  125.1 16.4 %all-reduce.5 = (f32[]{:T(128)}, f32[]{:T(128)}) all-reduce(f32[]{:T(128)} %get-tuple-element.30, f32[]{:T(128)} %get-tuple-element.31), channel_id=1, replica_groups=mesh['row_0'=4,'row_1'=2,'col_0'=4,'col_1'=4] {'col_0'}, use_global_device_ids=true, to_apply=%region_3.0 | all-reduce | flops 2 | bytes 16 | tf_op jit(solution)/shard_map/psum | solution.py:30
  141.4 12.5 %all-reduce.2 = (f32[]{:T(128)}, f32[]{:T(128)}) all-reduce(f32[]{:T(128)} %get-tuple-element.18, f32[]{:T(128)} %get-tuple-element.19), channel_id=1, replica_groups=mesh['row_0'=4,'row_1'=2,'col_0'=4,'col_1'=4] {'col_1'}, use_global_device_ids=true, to_apply=%region_4.0 | all-reduce | flops 2 | bytes 16 | tf_op jit(solution)/shard_map/psum | solution.py:30
  155.2 1.3 collective-permute-start.16
  156.5 1.3 collective-permute-start.17
  157.8 1.8 collective-permute-done.17
  159.7 1.9 collective-permute-start.18
  161.6 4.6 %collective-permute-start.19 = (f32[94,15]{1,0:T(8,128)S(1)}, f32[94,15]{1,0:T(8,128)S(1)}, u32[]{:S(2)}, u32[]{:S(2)}) collective-permute-start(f32[94,15]{1,0:T(8,128)S(1)} %get-tuple-element.112), channel_id=1, source_target_pairs={{1,0},{2,1},{3,2},{4,3},{5,4},{6,5},{7,6},{8,7},{9,8},{10,9},{11,1... | collective-permute-start | bytes 16928 | tf_op jit(solution)/shard_map/ppermute | solution.py:23
  166.2 1.5 collective-permute-done.19
  167.9 1.2 fusion.196
  171.4 1.2 convolution_add_fusion.117
  172.6 1.2 convolution_add_fusion.116
  176.0 1.2 convolution_add_fusion.113
  184.5 1.3 collective-permute-start.21
  185.8 3.2 collective-permute-start.20
  190.0 3.7 %collective-permute-start.23 = (f32[94,15]{1,0:T(8,128)S(1)}, f32[94,15]{1,0:T(8,128)S(1)}, u32[]{:S(2)}, u32[]{:S(2)}) collective-permute-start(f32[94,15]{1,0:T(8,128)S(1)} %get-tuple-element.107), channel_id=1, source_target_pairs={{1,0},{2,1},{3,2},{4,3},{5,4},{6,5},{7,6},{8,7},{9,8},{10,9},{11,1... | collective-permute-start | bytes 16928 | tf_op jit(solution)/shard_map/ppermute | solution.py:23
  193.7 2.3 collective-permute-start.22
  196.0 3.8 %collective-permute-done.22 = f32[94,15]{1,0:T(8,128)S(1)} collective-permute-done((f32[94,15]{1,0:T(8,128)S(1)}, f32[94,15]{1,0:T(8,128)S(1)}, u32[]{:S(2)}, u32[]{:S(2)}) %collective-permute-start.22) | collective-permute-done | bytes 5672 | tf_op jit(solution)/shard_map/ppermute | solution.py:22
  208.4 1.4 multiply_reduce_fusion.2
  209.8 12.8 %all-reduce.7 = (f32[]{:T(128)}, f32[]{:T(128)}) all-reduce(f32[]{:T(128)} %get-tuple-element.5, f32[]{:T(128)} %get-tuple-element.4), channel_id=1, replica_groups=mesh['row_0'=4,'row_1'=2,'col_0'=4,'col_1'=4] {'row_0'}, use_global_device_ids=true, to_apply=%region_11.0 | all-reduce | flops 2 | bytes 16 | tf_op jit(solution)/shard_map/psum | solution.py:30
  222.5 3.1 all-reduce.10
  225.7 10.3 %all-reduce.4 = (f32[]{:T(128)}, f32[]{:T(128)}) all-reduce(f32[]{:T(128)} %get-tuple-element.28, f32[]{:T(128)} %get-tuple-element.29), channel_id=1, replica_groups=mesh['row_0'=4,'row_1'=2,'col_0'=4,'col_1'=4] {'col_0'}, use_global_device_ids=true, to_apply=%region_13.0 | all-reduce | flops 2 | bytes 16 | tf_op jit(solution)/shard_map/psum | solution.py:30
  236.0 12.5 %all-reduce.1 = (f32[]{:T(128)}, f32[]{:T(128)}) all-reduce(f32[]{:T(128)} %get-tuple-element.16, f32[]{:T(128)} %get-tuple-element.17), channel_id=1, replica_groups=mesh['row_0'=4,'row_1'=2,'col_0'=4,'col_1'=4] {'col_1'}, use_global_device_ids=true, to_apply=%region_14.0 | all-reduce | flops 2 | bytes 16 | tf_op jit(solution)/shard_map/psum | solution.py:30
  253.7 1.3 collective-permute-start.24
  255.0 1.3 collective-permute-start.25
  256.3 2.4 collective-permute-done.25
  258.8 1.9 collective-permute-start.26
  260.7 4.3 %collective-permute-start.27 = (f32[94,15]{1,0:T(8,128)S(1)}, f32[94,15]{1,0:T(8,128)S(1)}, u32[]{:S(2)}, u32[]{:S(2)}) collective-permute-start(f32[94,15]{1,0:T(8,128)S(1)} %get-tuple-element.104), channel_id=1, source_target_pairs={{1,0},{2,1},{3,2},{4,3},{5,4},{6,5},{7,6},{8,7},{9,8},{10,9},{11,1... | collective-permute-start | bytes 16928 | tf_op jit(solution)/shard_map/ppermute | solution.py:23
  265.0 1.8 collective-permute-done.27
  268.2 1.2 convolution_add_fusion.59
  275.2 1.2 convolution_add_fusion.53
  283.6 1.3 collective-permute-start.29
  284.9 3.9 %collective-permute-start.28 = (f32[15,256]{1,0:T(8,128)S(1)}, f32[15,256]{1,0:T(8,128)S(1)}, u32[]{:S(2)}, u32[]{:S(2)}) collective-permute-start(f32[15,256]{1,0:T(8,128)S(1)} %bitcast.673), channel_id=1, source_target_pairs={{0,16},{16,32},{32,48},{48,64},{64,80},{80,96},{96,112},{1,17},{17... | collective-permute-start | bytes 46088 | tf_op jit(solution)/shard_map/ppermute | solution.py:22
  289.7 3.6 %collective-permute-start.31 = (f32[94,15]{1,0:T(8,128)S(1)}, f32[94,15]{1,0:T(8,128)S(1)}, u32[]{:S(2)}, u32[]{:S(2)}) collective-permute-start(f32[94,15]{1,0:T(8,128)S(1)} %get-tuple-element.99), channel_id=1, source_target_pairs={{1,0},{2,1},{3,2},{4,3},{5,4},{6,5},{7,6},{8,7},{9,8},{10,9},{11,1... | collective-permute-start | bytes 16928 | tf_op jit(solution)/shard_map/ppermute | solution.py:23
  293.4 2.5 collective-permute-start.30
  295.9 3.5 collective-permute-done.30
  308.8 13.0 %all-reduce.6 = (f32[]{:T(128)}, f32[]{:T(128)}) all-reduce(f32[]{:T(128)} %get-tuple-element.3, f32[]{:T(128)} %get-tuple-element.2), channel_id=1, replica_groups=mesh['row_0'=4,'row_1'=2,'col_0'=4,'col_1'=4] {'row_0'}, use_global_device_ids=true, to_apply=%region_21.0 | all-reduce | flops 2 | bytes 16 | tf_op jit(solution)/shard_map/psum | solution.py:30
  321.8 3.2 all-reduce.9
  324.9 11.2 %all-reduce.3 = (f32[]{:T(128)}, f32[]{:T(128)}) all-reduce(f32[]{:T(128)} %get-tuple-element.26, f32[]{:T(128)} %get-tuple-element.27), channel_id=1, replica_groups=mesh['row_0'=4,'row_1'=2,'col_0'=4,'col_1'=4] {'col_0'}, use_global_device_ids=true, to_apply=%region_23.0 | all-reduce | flops 2 | bytes 16 | tf_op jit(solution)/shard_map/psum | solution.py:30
  336.1 12.5 %all-reduce = (f32[]{:T(128)}, f32[]{:T(128)}) all-reduce(f32[]{:T(128)} %get-tuple-element.14, f32[]{:T(128)} %get-tuple-element.15), channel_id=1, replica_groups=mesh['row_0'=4,'row_1'=2,'col_0'=4,'col_1'=4] {'col_1'}, use_global_device_ids=true, to_apply=%region_24.0 | all-reduce | flops 2 | bytes 16 | tf_op jit(solution)/shard_map/psum | solution.py:30
  (444 shorter events, 88.4 us)
Async XLA Ops:
  1.4 9.9 %collective-permute-start = (f32[15,256]{1,0:T(8,128)S(1)}, f32[15,256]{1,0:T(8,128)S(1)}, u32[]{:S(2)}, u32[]{:S(2)}) collective-permute-start(f32[15,256]{1,0:T(8,128)S(1)} %get-tuple-element.145), channel_id=1, source_target_pairs={{0,16},{16,32},{32,48},{48,64},{64,80},{80,96},{96,112},{1,17},{17... | collective-permute-start | bytes 46088 | tf_op jit(solution)/shard_map/ppermute | solution.py:22
  3.1 8.2 %collective-permute-start.1 = (f32[15,256]{1,0:T(8,128)S(1)}, f32[15,256]{1,0:T(8,128)S(1)}, u32[]{:S(2)}, u32[]{:S(2)}) collective-permute-start(f32[15,256]{1,0:T(8,128)S(1)} %get-tuple-element.146), channel_id=1, source_target_pairs={{16,0},{32,16},{48,32},{64,48},{80,64},{96,80},{112,96},{17,1},{33... | collective-permute-start | bytes 46088 | tf_op jit(solution)/shard_map/ppermute | solution.py:23
  11.4 6.9 %collective-permute-start.3 = (f32[94,15]{1,0:T(8,128)S(1)}, f32[94,15]{1,0:T(8,128)S(1)}, u32[]{:S(2)}, u32[]{:S(2)}) collective-permute-start(f32[94,15]{1,0:T(8,128)S(1)} %get-tuple-element.127), channel_id=1, source_target_pairs={{1,0},{2,1},{3,2},{4,3},{5,4},{6,5},{7,6},{8,7},{9,8},{10,9},{11,1... | collective-permute-start | bytes 16928 | tf_op jit(solution)/shard_map/ppermute | solution.py:23
  13.4 6.0 %collective-permute-start.2 = (f32[94,15]{1,0:T(8,128)S(1)}, f32[94,15]{1,0:T(8,128)S(1)}, u32[]{:S(2)}, u32[]{:S(2)}) collective-permute-start(f32[94,15]{1,0:T(8,128)S(1)} %get-tuple-element.128), channel_id=1, source_target_pairs={{0,1},{1,2},{2,3},{3,4},{4,5},{5,6},{6,7},{7,8},{8,9},{9,10},{10,1... | collective-permute-start | bytes 16928 | tf_op jit(solution)/shard_map/ppermute | solution.py:22
  18.2 55.3 %copy-start.44 = (f32[1,158,128]{2,0,1:T(1,128)}, f32[1,158,128]{2,0,1:T(1,128)S(1)}, u32[]{:S(2)}) copy-start(f32[1,158,128]{2,0,1:T(1,128)S(1)} %get-tuple-element.96) | copy-start | bytes 242692
  18.2 55.6 %copy-start.43 = (f32[1,158,128]{2,0,1:T(1,128)}, f32[1,158,128]{2,0,1:T(1,128)S(1)}, u32[]{:S(2)}) copy-start(f32[1,158,128]{2,0,1:T(1,128)S(1)} %get-tuple-element.95) | copy-start | bytes 242692
  18.2 55.8 %copy-start.42 = (f32[1,158,128]{2,0,1:T(1,128)}, f32[1,158,128]{2,0,1:T(1,128)S(1)}, u32[]{:S(2)}) copy-start(f32[1,158,128]{2,0,1:T(1,128)S(1)} %get-tuple-element.94) | copy-start | bytes 242692
  18.2 56.1 %copy-start.41 = (f32[1,158,128]{2,0,1:T(1,128)}, f32[1,158,128]{2,0,1:T(1,128)S(1)}, u32[]{:S(2)}) copy-start(f32[1,158,128]{2,0,1:T(1,128)S(1)} %get-tuple-element.93) | copy-start | bytes 242692
  18.3 56.4 %copy-start.40 = (f32[1,158,128]{2,0,1:T(1,128)}, f32[1,158,128]{2,0,1:T(1,128)S(1)}, u32[]{:S(2)}) copy-start(f32[1,158,128]{2,0,1:T(1,128)S(1)} %get-tuple-element.92) | copy-start | bytes 242692
  18.3 56.6 %copy-start.39 = (f32[1,158,128]{2,0,1:T(1,128)}, f32[1,158,128]{2,0,1:T(1,128)S(1)}, u32[]{:S(2)}) copy-start(f32[1,158,128]{2,0,1:T(1,128)S(1)} %get-tuple-element.91) | copy-start | bytes 242692
  18.3 56.9 %copy-start.38 = (f32[1,158,128]{2,0,1:T(1,128)}, f32[1,158,128]{2,0,1:T(1,128)S(1)}, u32[]{:S(2)}) copy-start(f32[1,158,128]{2,0,1:T(1,128)S(1)} %get-tuple-element.90) | copy-start | bytes 242692
  18.3 57.2 %copy-start.37 = (f32[1,158,128]{2,0,1:T(1,128)}, f32[1,158,128]{2,0,1:T(1,128)S(1)}, u32[]{:S(2)}) copy-start(f32[1,158,128]{2,0,1:T(1,128)S(1)} %get-tuple-element.89) | copy-start | bytes 242692
  18.3 57.4 %copy-start.33 = (f32[1,158,128]{2,0,1:T(1,128)}, f32[1,158,128]{2,0,1:T(1,128)S(1)}, u32[]{:S(2)}) copy-start(f32[1,158,128]{2,0,1:T(1,128)S(1)} %get-tuple-element.88) | copy-start | bytes 242692
  18.3 57.7 %copy-start.27 = (f32[1,158,128]{2,0,1:T(1,128)}, f32[1,158,128]{2,0,1:T(1,128)S(1)}, u32[]{:S(2)}) copy-start(f32[1,158,128]{2,0,1:T(1,128)S(1)} %get-tuple-element.87) | copy-start | bytes 242692
  18.3 58.0 %copy-start.21 = (f32[1,158,128]{2,0,1:T(1,128)}, f32[1,158,128]{2,0,1:T(1,128)S(1)}, u32[]{:S(2)}) copy-start(f32[1,158,128]{2,0,1:T(1,128)S(1)} %get-tuple-element.86) | copy-start | bytes 242692
  18.3 58.3 %copy-start.15 = (f32[1,158,128]{2,0,1:T(1,128)}, f32[1,158,128]{2,0,1:T(1,128)S(1)}, u32[]{:S(2)}) copy-start(f32[1,158,128]{2,0,1:T(1,128)S(1)} %get-tuple-element.85) | copy-start | bytes 242692
  28.0 5.8 %collective-permute-start.5 = (f32[15,256]{1,0:T(8,128)S(1)}, f32[15,256]{1,0:T(8,128)S(1)}, u32[]{:S(2)}, u32[]{:S(2)}) collective-permute-start(f32[15,256]{1,0:T(8,128)S(1)} %bitcast.677), channel_id=1, source_target_pairs={{16,0},{32,16},{48,32},{64,48},{80,64},{96,80},{112,96},{17,1},{33... | collective-permute-start | bytes 46088 | tf_op jit(solution)/shard_map/ppermute | solution.py:23
  29.3 5.3 %collective-permute-start.4 = (f32[15,256]{1,0:T(8,128)S(1)}, f32[15,256]{1,0:T(8,128)S(1)}, u32[]{:S(2)}, u32[]{:S(2)}) collective-permute-start(f32[15,256]{1,0:T(8,128)S(1)} %bitcast.674), channel_id=1, source_target_pairs={{0,16},{16,32},{32,48},{48,64},{64,80},{80,96},{96,112},{1,17},{17... | collective-permute-start | bytes 46088 | tf_op jit(solution)/shard_map/ppermute | solution.py:22
  34.7 6.9 %collective-permute-start.7 = (f32[94,15]{1,0:T(8,128)S(1)}, f32[94,15]{1,0:T(8,128)S(1)}, u32[]{:S(2)}, u32[]{:S(2)}) collective-permute-start(f32[94,15]{1,0:T(8,128)S(1)} %get-tuple-element.123), channel_id=1, source_target_pairs={{1,0},{2,1},{3,2},{4,3},{5,4},{6,5},{7,6},{8,7},{9,8},{10,9},{11,1... | collective-permute-start | bytes 16928 | tf_op jit(solution)/shard_map/ppermute | solution.py:23
  36.6 6.0 %collective-permute-start.6 = (f32[94,15]{1,0:T(8,128)S(1)}, f32[94,15]{1,0:T(8,128)S(1)}, u32[]{:S(2)}, u32[]{:S(2)}) collective-permute-start(f32[94,15]{1,0:T(8,128)S(1)} %get-tuple-element.124), channel_id=1, source_target_pairs={{0,1},{1,2},{2,3},{3,4},{4,5},{5,6},{6,7},{7,8},{8,9},{9,10},{10,1... | collective-permute-start | bytes 16928 | tf_op jit(solution)/shard_map/ppermute | solution.py:22
  41.5 56.8 %copy-start.34 = (f32[1,158,128]{2,0,1:T(1,128)}, f32[1,158,128]{2,0,1:T(1,128)S(1)}, u32[]{:S(2)}) copy-start(f32[1,158,128]{2,0,1:T(1,128)S(1)} %get-tuple-element.65) | copy-start | bytes 242692
  41.5 57.1 %copy-start.30 = (f32[1,158,128]{2,0,1:T(1,128)}, f32[1,158,128]{2,0,1:T(1,128)S(1)}, u32[]{:S(2)}) copy-start(f32[1,158,128]{2,0,1:T(1,128)S(1)} %get-tuple-element.64) | copy-start | bytes 242692
  41.5 57.4 %copy-start.24 = (f32[1,158,128]{2,0,1:T(1,128)}, f32[1,158,128]{2,0,1:T(1,128)S(1)}, u32[]{:S(2)}) copy-start(f32[1,158,128]{2,0,1:T(1,128)S(1)} %get-tuple-element.63) | copy-start | bytes 242692
  41.5 57.6 %copy-start.18 = (f32[1,158,128]{2,0,1:T(1,128)}, f32[1,158,128]{2,0,1:T(1,128)S(1)}, u32[]{:S(2)}) copy-start(f32[1,158,128]{2,0,1:T(1,128)S(1)} %get-tuple-element.62) | copy-start | bytes 242692
  41.5 57.9 %copy-start.12 = (f32[1,158,128]{2,0,1:T(1,128)}, f32[1,158,128]{2,0,1:T(1,128)S(1)}, u32[]{:S(2)}) copy-start(f32[1,158,128]{2,0,1:T(1,128)S(1)} %get-tuple-element.61) | copy-start | bytes 242692
  41.5 58.2 %copy-start.9 = (f32[1,158,128]{2,0,1:T(1,128)}, f32[1,158,128]{2,0,1:T(1,128)S(1)}, u32[]{:S(2)}) copy-start(f32[1,158,128]{2,0,1:T(1,128)S(1)} %get-tuple-element.60) | copy-start | bytes 242692
  41.6 58.4 %copy-start.6 = (f32[1,158,128]{2,0,1:T(1,128)}, f32[1,158,128]{2,0,1:T(1,128)S(1)}, u32[]{:S(2)}) copy-start(f32[1,158,128]{2,0,1:T(1,128)S(1)} %get-tuple-element.59) | copy-start | bytes 242692
  41.6 58.7 %copy-start.3 = (f32[1,158,128]{2,0,1:T(1,128)}, f32[1,158,128]{2,0,1:T(1,128)S(1)}, u32[]{:S(2)}) copy-start(f32[1,158,128]{2,0,1:T(1,128)S(1)} %get-tuple-element.58) | copy-start | bytes 242692
  41.6 59.0 %copy-start = (f32[1,158,128]{2,0,1:T(1,128)}, f32[1,158,128]{2,0,1:T(1,128)S(1)}, u32[]{:S(2)}) copy-start(f32[1,158,128]{2,0,1:T(1,128)S(1)} %get-tuple-element.57) | copy-start | bytes 242692
  51.3 5.2 %collective-permute-start.8 = (f32[15,256]{1,0:T(8,128)S(1)}, f32[15,256]{1,0:T(8,128)S(1)}, u32[]{:S(2)}, u32[]{:S(2)}) collective-permute-start(f32[15,256]{1,0:T(8,128)S(1)} %get-tuple-element.141), channel_id=1, source_target_pairs={{0,16},{16,32},{32,48},{48,64},{64,80},{80,96},{96,112},{1,17},{17... | collective-permute-start | bytes 46088 | tf_op jit(solution)/shard_map/ppermute | solution.py:22
  55.2 6.0 %collective-permute-start.9 = (f32[15,256]{1,0:T(8,128)S(1)}, f32[15,256]{1,0:T(8,128)S(1)}, u32[]{:S(2)}, u32[]{:S(2)}) collective-permute-start(f32[15,256]{1,0:T(8,128)S(1)} %get-tuple-element.142), channel_id=1, source_target_pairs={{16,0},{32,16},{48,32},{64,48},{80,64},{96,80},{112,96},{17,1},{33... | collective-permute-start | bytes 46088 | tf_op jit(solution)/shard_map/ppermute | solution.py:23
  61.3 6.1 %collective-permute-start.10 = (f32[94,15]{1,0:T(8,128)S(1)}, f32[94,15]{1,0:T(8,128)S(1)}, u32[]{:S(2)}, u32[]{:S(2)}) collective-permute-start(f32[94,15]{1,0:T(8,128)S(1)} %get-tuple-element.119), channel_id=1, source_target_pairs={{0,1},{1,2},{2,3},{3,4},{4,5},{5,6},{6,7},{7,8},{8,9},{9,10},{10,1... | collective-permute-start | bytes 16928 | tf_op jit(solution)/shard_map/ppermute | solution.py:22
  65.3 8.0 %collective-permute-start.11 = (f32[94,15]{1,0:T(8,128)S(1)}, f32[94,15]{1,0:T(8,128)S(1)}, u32[]{:S(2)}, u32[]{:S(2)}) collective-permute-start(f32[94,15]{1,0:T(8,128)S(1)} %get-tuple-element.120), channel_id=1, source_target_pairs={{1,0},{2,1},{3,2},{4,3},{5,4},{6,5},{7,6},{8,7},{9,8},{10,9},{11,1... | collective-permute-start | bytes 16928 | tf_op jit(solution)/shard_map/ppermute | solution.py:23
  82.1 5.2 %collective-permute-start.13 = (f32[15,256]{1,0:T(8,128)S(1)}, f32[15,256]{1,0:T(8,128)S(1)}, u32[]{:S(2)}, u32[]{:S(2)}) collective-permute-start(f32[15,256]{1,0:T(8,128)S(1)} %bitcast.678), channel_id=1, source_target_pairs={{16,0},{32,16},{48,32},{64,48},{80,64},{96,80},{112,96},{17,1},{33... | collective-permute-start | bytes 46088 | tf_op jit(solution)/shard_map/ppermute | solution.py:23
  83.4 4.7 %collective-permute-start.12 = (f32[15,256]{1,0:T(8,128)S(1)}, f32[15,256]{1,0:T(8,128)S(1)}, u32[]{:S(2)}, u32[]{:S(2)}) collective-permute-start(f32[15,256]{1,0:T(8,128)S(1)} %bitcast.675), channel_id=1, source_target_pairs={{0,16},{16,32},{32,48},{48,64},{64,80},{80,96},{96,112},{1,17},{17... | collective-permute-start | bytes 46088 | tf_op jit(solution)/shard_map/ppermute | solution.py:22
  88.1 8.6 %collective-permute-start.15 = (f32[94,15]{1,0:T(8,128)S(1)}, f32[94,15]{1,0:T(8,128)S(1)}, u32[]{:S(2)}, u32[]{:S(2)}) collective-permute-start(f32[94,15]{1,0:T(8,128)S(1)} %get-tuple-element.115), channel_id=1, source_target_pairs={{1,0},{2,1},{3,2},{4,3},{5,4},{6,5},{7,6},{8,7},{9,8},{10,9},{11,1... | collective-permute-start | bytes 16928 | tf_op jit(solution)/shard_map/ppermute | solution.py:23
  90.1 8.1 %collective-permute-start.14 = (f32[94,15]{1,0:T(8,128)S(1)}, f32[94,15]{1,0:T(8,128)S(1)}, u32[]{:S(2)}, u32[]{:S(2)}) collective-permute-start(f32[94,15]{1,0:T(8,128)S(1)} %get-tuple-element.116), channel_id=1, source_target_pairs={{0,1},{1,2},{2,3},{3,4},{4,5},{5,6},{6,7},{7,8},{8,9},{9,10},{10,1... | collective-permute-start | bytes 16928 | tf_op jit(solution)/shard_map/ppermute | solution.py:22
  107.6 70.8 %copy-start.47 = (f32[64,256]{1,0:T(8,128)}, f32[64,256]{1,0:T(8,128)S(1)}, u32[]{:S(2)}) copy-start(f32[64,256]{1,0:T(8,128)S(1)} %get-tuple-element.34) | copy-start | bytes 196612
  155.1 23.2 %copy-start.28 = (f32[1,158,128]{2,0,1:T(1,128)S(1)}, f32[1,158,128]{2,0,1:T(1,128)}, u32[]{:S(2)}) copy-start(f32[1,158,128]{2,0,1:T(1,128)} %copy-done.27) | copy-start | bytes 242692
  155.2 2.6 collective-permute-start.16
  156.5 3.1 collective-permute-start.17
  159.6 19.1 %copy-start.22 = (f32[1,158,128]{2,0,1:T(1,128)S(1)}, f32[1,158,128]{2,0,1:T(1,128)}, u32[]{:S(2)}) copy-start(f32[1,158,128]{2,0,1:T(1,128)} %copy-done.21) | copy-start | bytes 242692
  159.7 6.5 %collective-permute-start.18 = (f32[94,15]{1,0:T(8,128)S(1)}, f32[94,15]{1,0:T(8,128)S(1)}, u32[]{:S(2)}, u32[]{:S(2)}) collective-permute-start(f32[94,15]{1,0:T(8,128)S(1)} %get-tuple-element.111), channel_id=1, source_target_pairs={{0,1},{1,2},{2,3},{3,4},{4,5},{5,6},{6,7},{7,8},{8,9},{9,10},{10,1... | collective-permute-start | bytes 16928 | tf_op jit(solution)/shard_map/ppermute | solution.py:22
  161.6 6.1 %collective-permute-start.19 = (f32[94,15]{1,0:T(8,128)S(1)}, f32[94,15]{1,0:T(8,128)S(1)}, u32[]{:S(2)}, u32[]{:S(2)}) collective-permute-start(f32[94,15]{1,0:T(8,128)S(1)} %get-tuple-element.112), channel_id=1, source_target_pairs={{1,0},{2,1},{3,2},{4,3},{5,4},{6,5},{7,6},{8,7},{9,8},{10,9},{11,1... | collective-permute-start | bytes 16928 | tf_op jit(solution)/shard_map/ppermute | solution.py:23
  184.5 4.5 %collective-permute-start.21 = (f32[15,256]{1,0:T(8,128)S(1)}, f32[15,256]{1,0:T(8,128)S(1)}, u32[]{:S(2)}, u32[]{:S(2)}) collective-permute-start(f32[15,256]{1,0:T(8,128)S(1)} %bitcast.679), channel_id=1, source_target_pairs={{16,0},{32,16},{48,32},{64,48},{80,64},{96,80},{112,96},{17,1},{33... | collective-permute-start | bytes 46088 | tf_op jit(solution)/shard_map/ppermute | solution.py:23
  185.8 4.1 %collective-permute-start.20 = (f32[15,256]{1,0:T(8,128)S(1)}, f32[15,256]{1,0:T(8,128)S(1)}, u32[]{:S(2)}, u32[]{:S(2)}) collective-permute-start(f32[15,256]{1,0:T(8,128)S(1)} %bitcast.676), channel_id=1, source_target_pairs={{0,16},{16,32},{32,48},{48,64},{64,80},{80,96},{96,112},{1,17},{17... | collective-permute-start | bytes 46088 | tf_op jit(solution)/shard_map/ppermute | solution.py:22
  190.0 6.0 %collective-permute-start.23 = (f32[94,15]{1,0:T(8,128)S(1)}, f32[94,15]{1,0:T(8,128)S(1)}, u32[]{:S(2)}, u32[]{:S(2)}) collective-permute-start(f32[94,15]{1,0:T(8,128)S(1)} %get-tuple-element.107), channel_id=1, source_target_pairs={{1,0},{2,1},{3,2},{4,3},{5,4},{6,5},{7,6},{8,7},{9,8},{10,9},{11,1... | collective-permute-start | bytes 16928 | tf_op jit(solution)/shard_map/ppermute | solution.py:23
  193.7 6.1 %collective-permute-start.22 = (f32[94,15]{1,0:T(8,128)S(1)}, f32[94,15]{1,0:T(8,128)S(1)}, u32[]{:S(2)}, u32[]{:S(2)}) collective-permute-start(f32[94,15]{1,0:T(8,128)S(1)} %get-tuple-element.108), channel_id=1, source_target_pairs={{0,1},{1,2},{2,3},{3,4},{4,5},{5,6},{6,7},{7,8},{8,9},{9,10},{10,1... | collective-permute-start | bytes 16928 | tf_op jit(solution)/shard_map/ppermute | solution.py:22
  252.7 24.8 %copy-start.29 = (f32[1,158,128]{2,0,1:T(1,128)S(1)}, f32[1,158,128]{2,0,1:T(1,128)}, u32[]{:S(2)}) copy-start(f32[1,158,128]{2,0,1:T(1,128)} %copy-done.27) | copy-start | bytes 242692
  253.7 2.6 collective-permute-start.24
  255.0 3.7 %collective-permute-start.25 = (f32[15,256]{1,0:T(8,128)S(1)}, f32[15,256]{1,0:T(8,128)S(1)}, u32[]{:S(2)}, u32[]{:S(2)}) collective-permute-start(f32[15,256]{1,0:T(8,128)S(1)} %get-tuple-element.134), channel_id=1, source_target_pairs={{16,0},{32,16},{48,32},{64,48},{80,64},{96,80},{112,96},{17,1},{33... | collective-permute-start | bytes 46088 | tf_op jit(solution)/shard_map/ppermute | solution.py:23
  258.7 19.0 %copy-start.23 = (f32[1,158,128]{2,0,1:T(1,128)S(1)}, f32[1,158,128]{2,0,1:T(1,128)}, u32[]{:S(2)}) copy-start(f32[1,158,128]{2,0,1:T(1,128)} %copy-done.21) | copy-start | bytes 242692
  258.8 6.2 %collective-permute-start.26 = (f32[94,15]{1,0:T(8,128)S(1)}, f32[94,15]{1,0:T(8,128)S(1)}, u32[]{:S(2)}, u32[]{:S(2)}) collective-permute-start(f32[94,15]{1,0:T(8,128)S(1)} %get-tuple-element.103), channel_id=1, source_target_pairs={{0,1},{1,2},{2,3},{3,4},{4,5},{5,6},{6,7},{7,8},{8,9},{9,10},{10,1... | collective-permute-start | bytes 16928 | tf_op jit(solution)/shard_map/ppermute | solution.py:22
  260.7 6.1 %collective-permute-start.27 = (f32[94,15]{1,0:T(8,128)S(1)}, f32[94,15]{1,0:T(8,128)S(1)}, u32[]{:S(2)}, u32[]{:S(2)}) collective-permute-start(f32[94,15]{1,0:T(8,128)S(1)} %get-tuple-element.104), channel_id=1, source_target_pairs={{1,0},{2,1},{3,2},{4,3},{5,4},{6,5},{7,6},{8,7},{9,8},{10,9},{11,1... | collective-permute-start | bytes 16928 | tf_op jit(solution)/shard_map/ppermute | solution.py:23
  281.0 18.8 %copy-start.32 = (f32[1,158,128]{2,0,1:T(1,128)S(1)}, f32[1,158,128]{2,0,1:T(1,128)}, u32[]{:S(2)}) copy-start(f32[1,158,128]{2,0,1:T(1,128)} %copy-done.30) | copy-start | bytes 242692
  281.3 18.8 %copy-start.26 = (f32[1,158,128]{2,0,1:T(1,128)S(1)}, f32[1,158,128]{2,0,1:T(1,128)}, u32[]{:S(2)}) copy-start(f32[1,158,128]{2,0,1:T(1,128)} %copy-done.24) | copy-start | bytes 242692
  281.6 18.8 %copy-start.20 = (f32[1,158,128]{2,0,1:T(1,128)S(1)}, f32[1,158,128]{2,0,1:T(1,128)}, u32[]{:S(2)}) copy-start(f32[1,158,128]{2,0,1:T(1,128)} %copy-done.18) | copy-start | bytes 242692
  283.6 5.2 %collective-permute-start.29 = (f32[15,256]{1,0:T(8,128)S(1)}, f32[15,256]{1,0:T(8,128)S(1)}, u32[]{:S(2)}, u32[]{:S(2)}) collective-permute-start(f32[15,256]{1,0:T(8,128)S(1)} %bitcast.680), channel_id=1, source_target_pairs={{16,0},{32,16},{48,32},{64,48},{80,64},{96,80},{112,96},{17,1},{33... | collective-permute-start | bytes 46088 | tf_op jit(solution)/shard_map/ppermute | solution.py:23
  284.9 4.7 %collective-permute-start.28 = (f32[15,256]{1,0:T(8,128)S(1)}, f32[15,256]{1,0:T(8,128)S(1)}, u32[]{:S(2)}, u32[]{:S(2)}) collective-permute-start(f32[15,256]{1,0:T(8,128)S(1)} %bitcast.673), channel_id=1, source_target_pairs={{0,16},{16,32},{32,48},{48,64},{64,80},{80,96},{96,112},{1,17},{17... | collective-permute-start | bytes 46088 | tf_op jit(solution)/shard_map/ppermute | solution.py:22
  289.7 6.1 %collective-permute-start.31 = (f32[94,15]{1,0:T(8,128)S(1)}, f32[94,15]{1,0:T(8,128)S(1)}, u32[]{:S(2)}, u32[]{:S(2)}) collective-permute-start(f32[94,15]{1,0:T(8,128)S(1)} %get-tuple-element.99), channel_id=1, source_target_pairs={{1,0},{2,1},{3,2},{4,3},{5,4},{6,5},{7,6},{8,7},{9,8},{10,9},{11,1... | collective-permute-start | bytes 16928 | tf_op jit(solution)/shard_map/ppermute | solution.py:23
  293.4 6.0 %collective-permute-start.30 = (f32[94,15]{1,0:T(8,128)S(1)}, f32[94,15]{1,0:T(8,128)S(1)}, u32[]{:S(2)}, u32[]{:S(2)}) collective-permute-start(f32[94,15]{1,0:T(8,128)S(1)} %get-tuple-element.100), channel_id=1, source_target_pairs={{0,1},{1,2},{2,3},{3,4},{4,5},{5,6},{6,7},{7,8},{8,9},{9,10},{10,1... | collective-permute-start | bytes 16928 | tf_op jit(solution)/shard_map/ppermute | solution.py:22
  304.7 47.8 %copy-start.46 = (f32[64,256]{1,0:T(8,128)S(1)}, f32[64,256]{1,0:T(8,128)}, u32[]{:S(2)}) copy-start(f32[64,256]{1,0:T(8,128)} %param.4) | copy-start | bytes 196612
  304.7 47.8 %copy-start.48 = (f32[64,256]{1,0:T(8,128)S(1)}, f32[64,256]{1,0:T(8,128)}, u32[]{:S(2)}) copy-start(f32[64,256]{1,0:T(8,128)} %copy-done.47) | copy-start | bytes 196612
  304.7 47.8 %copy-start.49 = (f32[64,256]{1,0:T(8,128)S(1)}, f32[64,256]{1,0:T(8,128)}, u32[]{:S(2)}) copy-start(f32[64,256]{1,0:T(8,128)} %get-tuple-element.33) | copy-start | bytes 196612
  (19 other events, 318.2 us)
where the time goes:
time: 360 us; the launch traced here: 353 us
  blocking collectives  125 us (35%)
  starting transfers between devices  85.5 us (24%)
  matrix products  84.5 us (23%)
  waiting for transfers between devices  32 us (9%)
  between operations  13.6 us (4%)
  local copies, waits for them, and re-layouts  7.13 us (2%)
  other arithmetic  5.84 us (2%)
    psum x12, blocking collectives, one_axis_at_a_time(): x = lax.psum(x, axis)  125 us
    dot_general x248, matrix products, correlate(): jnp.einsum('rnk,kj->rnj', window, tables[shift_row], precision=lax.Precis...  81.2 us
    ppermute x16, starting transfers between devices, with_halo(): before = lax.ppermute(last, axis, up)  51 us
    ppermute x16, starting transfers between devices, with_halo(): after = lax.ppermute(initial, axis, down)  34.4 us
    ppermute x16, waiting for transfers between devices, with_halo(): after = lax.ppermute(initial, axis, down)  18.1 us
    ppermute x16, waiting for transfers between devices, with_halo(): before = lax.ppermute(last, axis, up)  13.9 us
  transfers between devices with their start and end apart: 32, of which 15 were waited for; matrix products, arithmetic and copies ran while one was open for 2% of the time, Pallas kernels for 0%

commit v1 on v0

--- a/solution.py
+++ b/solution.py
@@ -27,7 +27,7 @@
 
 def one_axis_at_a_time(x, axes):
     for axis in axes:
-        x = lax.psum(x, axis)
+        x = jnp.sum(lax.all_gather(x, axis), axis=0)
     return x
 
 

time: 360 us -> 414 us (1.15)
  local copies, waits for them, and re-layouts: 7.13 us -> 44.1 us
  other arithmetic: 5.84 us -> 21.7 us
  matrix products: 84.5 us -> 92.5 us
  blocking collectives: 125 us -> 117 us
    psum x12 -> x0, blocking collectives: 125 us -> none  [one_axis_at_a_time(): x = lax.psum(x, axis)]
    unnamed x0 -> x12, blocking collectives: none -> 117 us
    unnamed x118 -> x188, local copies, waits for them, and re-layouts: 0.32 us -> 36.6 us
    reduce_sum x0 -> x24, other arithmetic: none -> 15.1 us  [one_axis_at_a_time(): x = jnp.sum(lax.all_gather(x, axis), axis=0)]
    dot_general x248, matrix products: 81.2 us -> 89.1 us  [correlate(): jnp.einsum('rnk,kj->rnj', window, tables[shift_row], precision=lax.Precis...]
where the time goes in v1:
time: 414 us; the launch traced here: 407 us
  blocking collectives  117 us (28%)
  matrix products  92.5 us (22%)
  starting transfers between devices  85.4 us (21%)
  local copies, waits for them, and re-layouts  44.1 us (11%)
  waiting for transfers between devices  31.9 us (8%)
  other arithmetic  21.7 us (5%)
  between operations  14.1 us (3%)
    unnamed x12, blocking collectives  117 us
    dot_general x248, matrix products, correlate(): jnp.einsum('rnk,kj->rnj', window, tables[shift_row], precision=lax.Precis...  89.1 us
    ppermute x16, starting transfers between devices, with_halo(): before = lax.ppermute(last, axis, up)  51.2 us
    unnamed x188, local copies, waits for them, and re-layouts  36.6 us
    ppermute x16, starting transfers between devices, with_halo(): after = lax.ppermute(initial, axis, down)  34.2 us
    ppermute x16, waiting for transfers between devices, with_halo(): after = lax.ppermute(initial, axis, down)  18.4 us
    reduce_sum x24, other arithmetic, one_axis_at_a_time(): x = jnp.sum(lax.all_gather(x, axis), axis=0)  15.1 us
    ppermute x16, waiting for transfers between devices, with_halo(): before = lax.ppermute(last, axis, up)  13.5 us
  transfers between devices with their start and end apart: 32, of which 15 were waited for; matrix products, arithmetic and copies ran while one was open for 2% of the time, Pallas kernels for 0%

profile of v1, /device:TPU:2, one launch (start us, length us, event | category | flops | bytes accessed | tf_op | source)
XLA Modules:
  0.0 406.5 jit_solution(6838787012146748974)
XLA Ops:
  1.4 1.7 collective-permute-start
  3.1 1.3 collective-permute-start.1
  5.2 2.0 fusion.2
  7.3 1.3 fusion.3
  8.6 1.3 fusion.1273
  10.0 1.3 fusion.1275
  11.4 1.9 collective-permute-start.3
  13.4 4.1 %collective-permute-start.2 = (f32[94,15]{1,0:T(8,128)S(1)}, f32[94,15]{1,0:T(8,128)S(1)}, u32[]{:S(2)}, u32[]{:S(2)}) collective-permute-start(f32[94,15]{1,0:T(8,128)S(1)} %get-tuple-element.128), channel_id=1, source_target_pairs={{0,1},{1,2},{2,3},{3,4},{4,5},{5,6},{6,7},{7,8},{8,9},{9,10},{10,1... | collective-permute-start | bytes 16928 | tf_op jit(solution)/shard_map/ppermute | solution.py:22
  28.0 1.3 collective-permute-start.5
  29.3 4.5 %collective-permute-start.4 = (f32[15,256]{1,0:T(8,128)S(1)}, f32[15,256]{1,0:T(8,128)S(1)}, u32[]{:S(2)}, u32[]{:S(2)}) collective-permute-start(f32[15,256]{1,0:T(8,128)S(1)} %bitcast.701), channel_id=1, source_target_pairs={{0,16},{16,32},{32,48},{48,64},{64,80},{80,96},{96,112},{1,17},{17... | collective-permute-start | bytes 46088 | tf_op jit(solution)/shard_map/ppermute | solution.py:22
  34.7 1.9 collective-permute-start.7
  36.6 4.1 %collective-permute-start.6 = (f32[94,15]{1,0:T(8,128)S(1)}, f32[94,15]{1,0:T(8,128)S(1)}, u32[]{:S(2)}, u32[]{:S(2)}) collective-permute-start(f32[94,15]{1,0:T(8,128)S(1)} %get-tuple-element.124), channel_id=1, source_target_pairs={{0,1},{1,2},{2,3},{3,4},{4,5},{5,6},{6,7},{7,8},{8,9},{9,10},{10,1... | collective-permute-start | bytes 16928 | tf_op jit(solution)/shard_map/ppermute | solution.py:22
  51.3 3.9 collective-permute-start.8
  56.6 4.7 %collective-permute-done.9 = f32[15,256]{1,0:T(8,128)S(1)} collective-permute-done((f32[15,256]{1,0:T(8,128)S(1)}, f32[15,256]{1,0:T(8,128)S(1)}, u32[]{:S(2)}, u32[]{:S(2)}) %collective-permute-start.9) | collective-permute-done | bytes 15392 | tf_op jit(solution)/shard_map/ppermute | solution.py:23
  61.4 3.9 collective-permute-start.10
  65.3 2.2 collective-permute-start.11
  67.5 5.8 %collective-permute-done.11 = f32[94,15]{1,0:T(8,128)S(1)} collective-permute-done((f32[94,15]{1,0:T(8,128)S(1)}, f32[94,15]{1,0:T(8,128)S(1)}, u32[]{:S(2)}, u32[]{:S(2)}) %collective-permute-start.11) | collective-permute-done | bytes 5672 | tf_op jit(solution)/shard_map/ppermute | solution.py:23
  82.6 1.3 collective-permute-start.13
  83.9 3.9 collective-permute-start.12
  89.3 1.9 collective-permute-start.15
  91.3 6.8 %collective-permute-start.14 = (f32[94,15]{1,0:T(8,128)}, f32[94,15]{1,0:T(8,128)}, u32[]{:S(2)}, u32[]{:S(2)}) collective-permute-start(f32[94,15]{1,0:T(8,128)} %get-tuple-element.116), channel_id=1, source_target_pairs={{0,1},{1,2},{2,3},{3,4},{4,5},{5,6},{6,7},{7,8},{8,9},{9,10},{10,1... | collective-permute-start | bytes 16928 | tf_op jit(solution)/shard_map/ppermute | solution.py:22
  117.8 1.3 dynamic-update-slice.4
  120.3 1.3 dynamic-slice.1
  121.6 13.8 %all-reduce.32 = (f32[4]{0:T(128)S(1)}, f32[4]{0:T(128)S(1)}) all-reduce(f32[4]{0:T(128)S(1)} %dynamic-update-slice, f32[4]{0:T(128)S(1)} %dynamic-update-slice.4), channel_id=1, replica_groups=mesh['row_0'=4,'row_1'=2,'col_0'=4,'col_1'=4] {'row_0'}, use_global_device_ids=true, to_apply=%add | all-reduce | flops 8 | bytes 64
  137.8 1.4 dynamic-update-slice.1
  140.5 2.4 all-reduce.35
  145.3 1.4 dynamic-update-slice.2
  147.9 15.8 %all-reduce.29 = (f32[4]{0:T(128)S(1)}, f32[4]{0:T(128)S(1)}) all-reduce(f32[4]{0:T(128)S(1)} %dynamic-update-slice.2, f32[4]{0:T(128)S(1)} %dynamic-update-slice.6), channel_id=1, replica_groups=mesh['row_0'=4,'row_1'=2,'col_0'=4,'col_1'=4] {'col_0'}, use_global_device_ids=true, to_apply=%add.2 | all-reduce | flops 8 | bytes 64
  166.2 1.3 dynamic-update-slice.3
  167.5 11.8 %all-reduce.26 = (f32[4]{0:T(128)S(1)}, f32[4]{0:T(128)S(1)}) all-reduce(f32[4]{0:T(128)S(1)} %dynamic-update-slice.3, f32[4]{0:T(128)S(1)} %dynamic-update-slice.7), channel_id=1, replica_groups=mesh['row_0'=4,'row_1'=2,'col_0'=4,'col_1'=4] {'col_1'}, use_global_device_ids=true, to_apply=%add.3 | all-reduce | flops 8 | bytes 64
  184.5 1.8 collective-permute-done.17
  186.4 1.9 collective-permute-start.18
  188.3 4.2 %collective-permute-start.19 = (f32[94,15]{1,0:T(8,128)S(1)}, f32[94,15]{1,0:T(8,128)S(1)}, u32[]{:S(2)}, u32[]{:S(2)}) collective-permute-start(f32[94,15]{1,0:T(8,128)S(1)} %get-tuple-element.112), channel_id=1, source_target_pairs={{1,0},{2,1},{3,2},{4,3},{5,4},{6,5},{7,6},{8,7},{9,8},{10,9},{11,1... | collective-permute-start | bytes 16928 | tf_op jit(solution)/shard_map/ppermute | solution.py:23
  192.6 1.9 collective-permute-done.19
  211.3 1.3 collective-permute-start.21
  212.6 3.2 collective-permute-start.20
  216.7 3.7 collective-permute-start.23
  220.4 2.3 collective-permute-start.22
  222.8 3.8 collective-permute-done.22
  235.1 1.4 multiply_reduce_fusion.2
  239.1 12.1 %all-reduce.31 = (f32[4]{0:T(128)S(1)}, f32[4]{0:T(128)S(1)}) all-reduce(f32[4]{0:T(128)S(1)} %dynamic-update-slice.8, f32[4]{0:T(128)S(1)} %dynamic-update-slice.12), channel_id=1, replica_groups=mesh['row_0'=4,'row_1'=2,'col_0'=4,'col_1'=4] {'row_0'}, use_global_device_ids=true, to_apply=%add.8 | all-reduce | flops 8 | bytes 64
  251.8 1.4 dynamic-update-slice.13
  253.9 1.4 dynamic-update-slice.9
  255.2 2.4 all-reduce.34
  258.3 1.4 dynamic-update-slice.14
  260.3 1.4 dynamic-update-slice.10
  261.7 9.7 %all-reduce.28 = (f32[4]{0:T(128)S(1)}, f32[4]{0:T(128)S(1)}) all-reduce(f32[4]{0:T(128)S(1)} %dynamic-update-slice.10, f32[4]{0:T(128)S(1)} %dynamic-update-slice.14), channel_id=1, replica_groups=mesh['row_0'=4,'row_1'=2,'col_0'=4,'col_1'=4] {'col_0'}, use_global_device_ids=true, to_apply=%add.10 | all-reduce | flops 8 | bytes 64
  275.2 11.8 %all-reduce.25 = (f32[4]{0:T(128)S(1)}, f32[4]{0:T(128)S(1)}) all-reduce(f32[4]{0:T(128)S(1)} %dynamic-update-slice.11, f32[4]{0:T(128)S(1)} %dynamic-update-slice.15), channel_id=1, replica_groups=mesh['row_0'=4,'row_1'=2,'col_0'=4,'col_1'=4] {'col_1'}, use_global_device_ids=true, to_apply=%add.11 | all-reduce | flops 8 | bytes 64
  296.3 2.4 collective-permute-done.25
  298.8 1.9 collective-permute-start.26
  300.8 4.3 %collective-permute-start.27 = (f32[94,15]{1,0:T(8,128)S(1)}, f32[94,15]{1,0:T(8,128)S(1)}, u32[]{:S(2)}, u32[]{:S(2)}) collective-permute-start(f32[94,15]{1,0:T(8,128)S(1)} %get-tuple-element.104), channel_id=1, source_target_pairs={{1,0},{2,1},{3,2},{4,3},{5,4},{6,5},{7,6},{8,7},{9,8},{10,9},{11,1... | collective-permute-start | bytes 16928 | tf_op jit(solution)/shard_map/ppermute | solution.py:23
  305.1 1.8 collective-permute-done.27
  325.0 3.9 collective-permute-start.28
  329.7 3.7 collective-permute-start.31
  333.4 2.5 collective-permute-start.30
  335.9 3.5 collective-permute-done.30
  351.3 12.3 %all-reduce.30 = (f32[4]{0:T(128)S(1)}, f32[4]{0:T(128)S(1)}) all-reduce(f32[4]{0:T(128)S(1)} %dynamic-update-slice.16, f32[4]{0:T(128)S(1)} %dynamic-update-slice.20), channel_id=1, replica_groups=mesh['row_0'=4,'row_1'=2,'col_0'=4,'col_1'=4] {'row_0'}, use_global_device_ids=true, to_apply=%add.16 | all-reduce | flops 8 | bytes 64
  364.3 1.4 dynamic-update-slice.21
  366.4 1.4 dynamic-update-slice.17
  367.7 2.4 all-reduce.33
  370.8 1.4 dynamic-update-slice.22
  372.9 1.4 dynamic-update-slice.18
  374.2 10.6 %all-reduce.27 = (f32[4]{0:T(128)S(1)}, f32[4]{0:T(128)S(1)}) all-reduce(f32[4]{0:T(128)S(1)} %dynamic-update-slice.18, f32[4]{0:T(128)S(1)} %dynamic-update-slice.22), channel_id=1, replica_groups=mesh['row_0'=4,'row_1'=2,'col_0'=4,'col_1'=4] {'col_0'}, use_global_device_ids=true, to_apply=%add.18 | all-reduce | flops 8 | bytes 64
  388.5 11.8 %all-reduce.24 = (f32[4]{0:T(128)S(1)}, f32[4]{0:T(128)S(1)}) all-reduce(f32[4]{0:T(128)S(1)} %dynamic-update-slice.19, f32[4]{0:T(128)S(1)} %dynamic-update-slice.23), channel_id=1, replica_groups=mesh['row_0'=4,'row_1'=2,'col_0'=4,'col_1'=4] {'col_1'}, use_global_device_ids=true, to_apply=%add.19 | all-reduce | flops 8 | bytes 64
  (538 shorter events, 147.2 us)
Async XLA Ops:
  1.4 9.9 %collective-permute-start = (f32[15,256]{1,0:T(8,128)S(1)}, f32[15,256]{1,0:T(8,128)S(1)}, u32[]{:S(2)}, u32[]{:S(2)}) collective-permute-start(f32[15,256]{1,0:T(8,128)S(1)} %get-tuple-element.145), channel_id=1, source_target_pairs={{0,16},{16,32},{32,48},{48,64},{64,80},{80,96},{96,112},{1,17},{17... | collective-permute-start | bytes 46088 | tf_op jit(solution)/shard_map/ppermute | solution.py:22
  3.1 8.2 %collective-permute-start.1 = (f32[15,256]{1,0:T(8,128)S(1)}, f32[15,256]{1,0:T(8,128)S(1)}, u32[]{:S(2)}, u32[]{:S(2)}) collective-permute-start(f32[15,256]{1,0:T(8,128)S(1)} %get-tuple-element.146), channel_id=1, source_target_pairs={{16,0},{32,16},{48,32},{64,48},{80,64},{96,80},{112,96},{17,1},{33... | collective-permute-start | bytes 46088 | tf_op jit(solution)/shard_map/ppermute | solution.py:23
  11.4 6.9 %collective-permute-start.3 = (f32[94,15]{1,0:T(8,128)S(1)}, f32[94,15]{1,0:T(8,128)S(1)}, u32[]{:S(2)}, u32[]{:S(2)}) collective-permute-start(f32[94,15]{1,0:T(8,128)S(1)} %get-tuple-element.127), channel_id=1, source_target_pairs={{1,0},{2,1},{3,2},{4,3},{5,4},{6,5},{7,6},{8,7},{9,8},{10,9},{11,1... | collective-permute-start | bytes 16928 | tf_op jit(solution)/shard_map/ppermute | solution.py:23
  13.4 6.0 %collective-permute-start.2 = (f32[94,15]{1,0:T(8,128)S(1)}, f32[94,15]{1,0:T(8,128)S(1)}, u32[]{:S(2)}, u32[]{:S(2)}) collective-permute-start(f32[94,15]{1,0:T(8,128)S(1)} %get-tuple-element.128), channel_id=1, source_target_pairs={{0,1},{1,2},{2,3},{3,4},{4,5},{5,6},{6,7},{7,8},{8,9},{9,10},{10,1... | collective-permute-start | bytes 16928 | tf_op jit(solution)/shard_map/ppermute | solution.py:22
  18.2 55.8 %copy-start.44 = (f32[1,158,128]{2,0,1:T(1,128)}, f32[1,158,128]{2,0,1:T(1,128)S(1)}, u32[]{:S(2)}) copy-start(f32[1,158,128]{2,0,1:T(1,128)S(1)} %get-tuple-element.96) | copy-start | bytes 242692
  18.2 56.1 %copy-start.43 = (f32[1,158,128]{2,0,1:T(1,128)}, f32[1,158,128]{2,0,1:T(1,128)S(1)}, u32[]{:S(2)}) copy-start(f32[1,158,128]{2,0,1:T(1,128)S(1)} %get-tuple-element.95) | copy-start | bytes 242692
  18.2 56.3 %copy-start.42 = (f32[1,158,128]{2,0,1:T(1,128)}, f32[1,158,128]{2,0,1:T(1,128)S(1)}, u32[]{:S(2)}) copy-start(f32[1,158,128]{2,0,1:T(1,128)S(1)} %get-tuple-element.94) | copy-start | bytes 242692
  18.2 56.6 %copy-start.41 = (f32[1,158,128]{2,0,1:T(1,128)}, f32[1,158,128]{2,0,1:T(1,128)S(1)}, u32[]{:S(2)}) copy-start(f32[1,158,128]{2,0,1:T(1,128)S(1)} %get-tuple-element.93) | copy-start | bytes 242692
  18.3 56.9 %copy-start.40 = (f32[1,158,128]{2,0,1:T(1,128)}, f32[1,158,128]{2,0,1:T(1,128)S(1)}, u32[]{:S(2)}) copy-start(f32[1,158,128]{2,0,1:T(1,128)S(1)} %get-tuple-element.92) | copy-start | bytes 242692
  18.3 57.2 %copy-start.39 = (f32[1,158,128]{2,0,1:T(1,128)}, f32[1,158,128]{2,0,1:T(1,128)S(1)}, u32[]{:S(2)}) copy-start(f32[1,158,128]{2,0,1:T(1,128)S(1)} %get-tuple-element.91) | copy-start | bytes 242692
  18.3 57.4 %copy-start.38 = (f32[1,158,128]{2,0,1:T(1,128)}, f32[1,158,128]{2,0,1:T(1,128)S(1)}, u32[]{:S(2)}) copy-start(f32[1,158,128]{2,0,1:T(1,128)S(1)} %get-tuple-element.90) | copy-start | bytes 242692
  18.3 57.7 %copy-start.37 = (f32[1,158,128]{2,0,1:T(1,128)}, f32[1,158,128]{2,0,1:T(1,128)S(1)}, u32[]{:S(2)}) copy-start(f32[1,158,128]{2,0,1:T(1,128)S(1)} %get-tuple-element.89) | copy-start | bytes 242692
  18.3 58.0 %copy-start.30 = (f32[1,158,128]{2,0,1:T(1,128)}, f32[1,158,128]{2,0,1:T(1,128)S(1)}, u32[]{:S(2)}) copy-start(f32[1,158,128]{2,0,1:T(1,128)S(1)} %get-tuple-element.88) | copy-start | bytes 242692
  18.3 58.2 %copy-start.24 = (f32[1,158,128]{2,0,1:T(1,128)}, f32[1,158,128]{2,0,1:T(1,128)S(1)}, u32[]{:S(2)}) copy-start(f32[1,158,128]{2,0,1:T(1,128)S(1)} %get-tuple-element.87) | copy-start | bytes 242692
  18.3 58.5 %copy-start.18 = (f32[1,158,128]{2,0,1:T(1,128)}, f32[1,158,128]{2,0,1:T(1,128)S(1)}, u32[]{:S(2)}) copy-start(f32[1,158,128]{2,0,1:T(1,128)S(1)} %get-tuple-element.86) | copy-start | bytes 242692
  18.3 58.8 %copy-start.12 = (f32[1,158,128]{2,0,1:T(1,128)}, f32[1,158,128]{2,0,1:T(1,128)S(1)}, u32[]{:S(2)}) copy-start(f32[1,158,128]{2,0,1:T(1,128)S(1)} %get-tuple-element.85) | copy-start | bytes 242692
  28.0 5.8 %collective-permute-start.5 = (f32[15,256]{1,0:T(8,128)S(1)}, f32[15,256]{1,0:T(8,128)S(1)}, u32[]{:S(2)}, u32[]{:S(2)}) collective-permute-start(f32[15,256]{1,0:T(8,128)S(1)} %bitcast.705), channel_id=1, source_target_pairs={{16,0},{32,16},{48,32},{64,48},{80,64},{96,80},{112,96},{17,1},{33... | collective-permute-start | bytes 46088 | tf_op jit(solution)/shard_map/ppermute | solution.py:23
  29.3 5.3 %collective-permute-start.4 = (f32[15,256]{1,0:T(8,128)S(1)}, f32[15,256]{1,0:T(8,128)S(1)}, u32[]{:S(2)}, u32[]{:S(2)}) collective-permute-start(f32[15,256]{1,0:T(8,128)S(1)} %bitcast.701), channel_id=1, source_target_pairs={{0,16},{16,32},{32,48},{48,64},{64,80},{80,96},{96,112},{1,17},{17... | collective-permute-start | bytes 46088 | tf_op jit(solution)/shard_map/ppermute | solution.py:22
  34.7 6.9 %collective-permute-start.7 = (f32[94,15]{1,0:T(8,128)S(1)}, f32[94,15]{1,0:T(8,128)S(1)}, u32[]{:S(2)}, u32[]{:S(2)}) collective-permute-start(f32[94,15]{1,0:T(8,128)S(1)} %get-tuple-element.123), channel_id=1, source_target_pairs={{1,0},{2,1},{3,2},{4,3},{5,4},{6,5},{7,6},{8,7},{9,8},{10,9},{11,1... | collective-permute-start | bytes 16928 | tf_op jit(solution)/shard_map/ppermute | solution.py:23
  36.6 6.0 %collective-permute-start.6 = (f32[94,15]{1,0:T(8,128)S(1)}, f32[94,15]{1,0:T(8,128)S(1)}, u32[]{:S(2)}, u32[]{:S(2)}) collective-permute-start(f32[94,15]{1,0:T(8,128)S(1)} %get-tuple-element.124), channel_id=1, source_target_pairs={{0,1},{1,2},{2,3},{3,4},{4,5},{5,6},{6,7},{7,8},{8,9},{9,10},{10,1... | collective-permute-start | bytes 16928 | tf_op jit(solution)/shard_map/ppermute | solution.py:22
  41.6 33.0 %copy-start = (f32[1,158,128]{2,0,1:T(1,128)}, f32[1,158,128]{2,0,1:T(1,128)S(1)}, u32[]{:S(2)}) copy-start(f32[1,158,128]{2,0,1:T(1,128)S(1)} %get-tuple-element.57) | copy-start | bytes 242692
  41.6 33.0 %copy-start.3 = (f32[1,158,128]{2,0,1:T(1,128)}, f32[1,158,128]{2,0,1:T(1,128)S(1)}, u32[]{:S(2)}) copy-start(f32[1,158,128]{2,0,1:T(1,128)S(1)} %get-tuple-element.58) | copy-start | bytes 242692
  41.6 33.0 %copy-start.6 = (f32[1,158,128]{2,0,1:T(1,128)}, f32[1,158,128]{2,0,1:T(1,128)S(1)}, u32[]{:S(2)}) copy-start(f32[1,158,128]{2,0,1:T(1,128)S(1)} %get-tuple-element.59) | copy-start | bytes 242692
  41.6 33.0 %copy-start.9 = (f32[1,158,128]{2,0,1:T(1,128)}, f32[1,158,128]{2,0,1:T(1,128)S(1)}, u32[]{:S(2)}) copy-start(f32[1,158,128]{2,0,1:T(1,128)S(1)} %get-tuple-element.60) | copy-start | bytes 242692
  51.3 5.2 %collective-permute-start.8 = (f32[15,256]{1,0:T(8,128)S(1)}, f32[15,256]{1,0:T(8,128)S(1)}, u32[]{:S(2)}, u32[]{:S(2)}) collective-permute-start(f32[15,256]{1,0:T(8,128)S(1)} %get-tuple-element.141), channel_id=1, source_target_pairs={{0,16},{16,32},{32,48},{48,64},{64,80},{80,96},{96,112},{1,17},{17... | collective-permute-start | bytes 46088 | tf_op jit(solution)/shard_map/ppermute | solution.py:22
  55.3 6.0 %collective-permute-start.9 = (f32[15,256]{1,0:T(8,128)S(1)}, f32[15,256]{1,0:T(8,128)S(1)}, u32[]{:S(2)}, u32[]{:S(2)}) collective-permute-start(f32[15,256]{1,0:T(8,128)S(1)} %get-tuple-element.142), channel_id=1, source_target_pairs={{16,0},{32,16},{48,32},{64,48},{80,64},{96,80},{112,96},{17,1},{33... | collective-permute-start | bytes 46088 | tf_op jit(solution)/shard_map/ppermute | solution.py:23
  56.6 20.3 %copy-start.54 = (f32[15,256]{1,0:T(8,128)}, f32[15,256]{1,0:T(8,128)S(1)}, u32[]{:S(2)}) copy-start(f32[15,256]{1,0:T(8,128)S(1)} %collective-permute-done.8) | copy-start | bytes 46084
  61.4 6.1 %collective-permute-start.10 = (f32[94,15]{1,0:T(8,128)S(1)}, f32[94,15]{1,0:T(8,128)S(1)}, u32[]{:S(2)}, u32[]{:S(2)}) collective-permute-start(f32[94,15]{1,0:T(8,128)S(1)} %get-tuple-element.119), channel_id=1, source_target_pairs={{0,1},{1,2},{2,3},{3,4},{4,5},{5,6},{6,7},{7,8},{8,9},{9,10},{10,1... | collective-permute-start | bytes 16928 | tf_op jit(solution)/shard_map/ppermute | solution.py:22
  65.3 8.0 %collective-permute-start.11 = (f32[94,15]{1,0:T(8,128)S(1)}, f32[94,15]{1,0:T(8,128)S(1)}, u32[]{:S(2)}, u32[]{:S(2)}) collective-permute-start(f32[94,15]{1,0:T(8,128)S(1)} %get-tuple-element.120), channel_id=1, source_target_pairs={{1,0},{2,1},{3,2},{4,3},{5,4},{6,5},{7,6},{8,7},{9,8},{10,9},{11,1... | collective-permute-start | bytes 16928 | tf_op jit(solution)/shard_map/ppermute | solution.py:23
  82.6 5.2 %collective-permute-start.13 = (f32[15,256]{1,0:T(8,128)S(1)}, f32[15,256]{1,0:T(8,128)S(1)}, u32[]{:S(2)}, u32[]{:S(2)}) collective-permute-start(f32[15,256]{1,0:T(8,128)S(1)} %bitcast.706), channel_id=1, source_target_pairs={{16,0},{32,16},{48,32},{64,48},{80,64},{96,80},{112,96},{17,1},{33... | collective-permute-start | bytes 46088 | tf_op jit(solution)/shard_map/ppermute | solution.py:23
  83.9 4.7 %collective-permute-start.12 = (f32[15,256]{1,0:T(8,128)S(1)}, f32[15,256]{1,0:T(8,128)S(1)}, u32[]{:S(2)}, u32[]{:S(2)}) collective-permute-start(f32[15,256]{1,0:T(8,128)S(1)} %bitcast.702), channel_id=1, source_target_pairs={{0,16},{16,32},{32,48},{48,64},{64,80},{80,96},{96,112},{1,17},{17... | collective-permute-start | bytes 46088 | tf_op jit(solution)/shard_map/ppermute | solution.py:22
  89.3 9.3 %collective-permute-start.15 = (f32[94,15]{1,0:T(8,128)}, f32[94,15]{1,0:T(8,128)}, u32[]{:S(2)}, u32[]{:S(2)}) collective-permute-start(f32[94,15]{1,0:T(8,128)} %get-tuple-element.115), channel_id=1, source_target_pairs={{1,0},{2,1},{3,2},{4,3},{5,4},{6,5},{7,6},{8,7},{9,8},{10,9},{11,1... | collective-permute-start | bytes 16928 | tf_op jit(solution)/shard_map/ppermute | solution.py:23
  91.3 8.4 %collective-permute-start.14 = (f32[94,15]{1,0:T(8,128)}, f32[94,15]{1,0:T(8,128)}, u32[]{:S(2)}, u32[]{:S(2)}) collective-permute-start(f32[94,15]{1,0:T(8,128)} %get-tuple-element.116), channel_id=1, source_target_pairs={{0,1},{1,2},{2,3},{3,4},{4,5},{5,6},{6,7},{7,8},{8,9},{9,10},{10,1... | collective-permute-start | bytes 16928 | tf_op jit(solution)/shard_map/ppermute | solution.py:22
  117.8 87.3 %copy-start.47 = (f32[64,256]{1,0:T(8,128)}, f32[64,256]{1,0:T(8,128)S(1)}, u32[]{:S(2)}) copy-start(f32[64,256]{1,0:T(8,128)S(1)} %get-tuple-element.34) | copy-start | bytes 196612
  181.9 23.2 %copy-start.25 = (f32[1,158,128]{2,0,1:T(1,128)S(1)}, f32[1,158,128]{2,0,1:T(1,128)}, u32[]{:S(2)}) copy-start(f32[1,158,128]{2,0,1:T(1,128)} %copy-done.24) | copy-start | bytes 242692
  181.9 2.6 collective-permute-start.16
  183.2 3.1 collective-permute-start.17
  186.3 19.1 %copy-start.19 = (f32[1,158,128]{2,0,1:T(1,128)S(1)}, f32[1,158,128]{2,0,1:T(1,128)}, u32[]{:S(2)}) copy-start(f32[1,158,128]{2,0,1:T(1,128)} %copy-done.18) | copy-start | bytes 242692
  186.4 6.2 %collective-permute-start.18 = (f32[94,15]{1,0:T(8,128)S(1)}, f32[94,15]{1,0:T(8,128)S(1)}, u32[]{:S(2)}, u32[]{:S(2)}) collective-permute-start(f32[94,15]{1,0:T(8,128)S(1)} %get-tuple-element.111), channel_id=1, source_target_pairs={{0,1},{1,2},{2,3},{3,4},{4,5},{5,6},{6,7},{7,8},{8,9},{9,10},{10,1... | collective-permute-start | bytes 16928 | tf_op jit(solution)/shard_map/ppermute | solution.py:22
  188.3 6.1 %collective-permute-start.19 = (f32[94,15]{1,0:T(8,128)S(1)}, f32[94,15]{1,0:T(8,128)S(1)}, u32[]{:S(2)}, u32[]{:S(2)}) collective-permute-start(f32[94,15]{1,0:T(8,128)S(1)} %get-tuple-element.112), channel_id=1, source_target_pairs={{1,0},{2,1},{3,2},{4,3},{5,4},{6,5},{7,6},{8,7},{9,8},{10,9},{11,1... | collective-permute-start | bytes 16928 | tf_op jit(solution)/shard_map/ppermute | solution.py:23
  211.3 4.5 %collective-permute-start.21 = (f32[15,256]{1,0:T(8,128)S(1)}, f32[15,256]{1,0:T(8,128)S(1)}, u32[]{:S(2)}, u32[]{:S(2)}) collective-permute-start(f32[15,256]{1,0:T(8,128)S(1)} %bitcast.707), channel_id=1, source_target_pairs={{16,0},{32,16},{48,32},{64,48},{80,64},{96,80},{112,96},{17,1},{33... | collective-permute-start | bytes 46088 | tf_op jit(solution)/shard_map/ppermute | solution.py:23
  212.6 4.0 collective-permute-start.20
  216.7 6.1 %collective-permute-start.23 = (f32[94,15]{1,0:T(8,128)S(1)}, f32[94,15]{1,0:T(8,128)S(1)}, u32[]{:S(2)}, u32[]{:S(2)}) collective-permute-start(f32[94,15]{1,0:T(8,128)S(1)} %get-tuple-element.107), channel_id=1, source_target_pairs={{1,0},{2,1},{3,2},{4,3},{5,4},{6,5},{7,6},{8,7},{9,8},{10,9},{11,1... | collective-permute-start | bytes 16928 | tf_op jit(solution)/shard_map/ppermute | solution.py:23
  220.4 6.1 %collective-permute-start.22 = (f32[94,15]{1,0:T(8,128)S(1)}, f32[94,15]{1,0:T(8,128)S(1)}, u32[]{:S(2)}, u32[]{:S(2)}) collective-permute-start(f32[94,15]{1,0:T(8,128)S(1)} %get-tuple-element.108), channel_id=1, source_target_pairs={{0,1},{1,2},{2,3},{3,4},{4,5},{5,6},{6,7},{7,8},{8,9},{9,10},{10,1... | collective-permute-start | bytes 16928 | tf_op jit(solution)/shard_map/ppermute | solution.py:22
  292.7 24.8 %copy-start.26 = (f32[1,158,128]{2,0,1:T(1,128)S(1)}, f32[1,158,128]{2,0,1:T(1,128)}, u32[]{:S(2)}) copy-start(f32[1,158,128]{2,0,1:T(1,128)} %copy-done.24) | copy-start | bytes 242692
  293.7 2.6 collective-permute-start.24
  295.0 3.7 collective-permute-start.25
  298.7 19.0 %copy-start.20 = (f32[1,158,128]{2,0,1:T(1,128)S(1)}, f32[1,158,128]{2,0,1:T(1,128)}, u32[]{:S(2)}) copy-start(f32[1,158,128]{2,0,1:T(1,128)} %copy-done.18) | copy-start | bytes 242692
  298.8 6.2 %collective-permute-start.26 = (f32[94,15]{1,0:T(8,128)S(1)}, f32[94,15]{1,0:T(8,128)S(1)}, u32[]{:S(2)}, u32[]{:S(2)}) collective-permute-start(f32[94,15]{1,0:T(8,128)S(1)} %get-tuple-element.103), channel_id=1, source_target_pairs={{0,1},{1,2},{2,3},{3,4},{4,5},{5,6},{6,7},{7,8},{8,9},{9,10},{10,1... | collective-permute-start | bytes 16928 | tf_op jit(solution)/shard_map/ppermute | solution.py:22
  300.8 6.1 %collective-permute-start.27 = (f32[94,15]{1,0:T(8,128)S(1)}, f32[94,15]{1,0:T(8,128)S(1)}, u32[]{:S(2)}, u32[]{:S(2)}) collective-permute-start(f32[94,15]{1,0:T(8,128)S(1)} %get-tuple-element.104), channel_id=1, source_target_pairs={{1,0},{2,1},{3,2},{4,3},{5,4},{6,5},{7,6},{8,7},{9,8},{10,9},{11,1... | collective-permute-start | bytes 16928 | tf_op jit(solution)/shard_map/ppermute | solution.py:23
  320.8 18.8 %copy-start.36 = (f32[1,158,128]{2,0,1:T(1,128)S(1)}, f32[1,158,128]{2,0,1:T(1,128)}, u32[]{:S(2)}) copy-start(f32[1,158,128]{2,0,1:T(1,128)} %copy-done.34) | copy-start | bytes 242692
  321.0 18.8 %copy-start.33 = (f32[1,158,128]{2,0,1:T(1,128)S(1)}, f32[1,158,128]{2,0,1:T(1,128)}, u32[]{:S(2)}) copy-start(f32[1,158,128]{2,0,1:T(1,128)} %copy-done.31) | copy-start | bytes 242692
  321.3 18.8 %copy-start.29 = (f32[1,158,128]{2,0,1:T(1,128)S(1)}, f32[1,158,128]{2,0,1:T(1,128)}, u32[]{:S(2)}) copy-start(f32[1,158,128]{2,0,1:T(1,128)} %copy-done.27) | copy-start | bytes 242692
  321.6 18.8 %copy-start.23 = (f32[1,158,128]{2,0,1:T(1,128)S(1)}, f32[1,158,128]{2,0,1:T(1,128)}, u32[]{:S(2)}) copy-start(f32[1,158,128]{2,0,1:T(1,128)} %copy-done.21) | copy-start | bytes 242692
  321.9 18.8 %copy-start.17 = (f32[1,158,128]{2,0,1:T(1,128)S(1)}, f32[1,158,128]{2,0,1:T(1,128)}, u32[]{:S(2)}) copy-start(f32[1,158,128]{2,0,1:T(1,128)} %copy-done.15) | copy-start | bytes 242692
  322.2 18.8 %copy-start.11 = (f32[1,158,128]{2,0,1:T(1,128)S(1)}, f32[1,158,128]{2,0,1:T(1,128)}, u32[]{:S(2)}) copy-start(f32[1,158,128]{2,0,1:T(1,128)} %copy-done.9) | copy-start | bytes 242692
  322.4 18.8 %copy-start.8 = (f32[1,158,128]{2,0,1:T(1,128)S(1)}, f32[1,158,128]{2,0,1:T(1,128)}, u32[]{:S(2)}) copy-start(f32[1,158,128]{2,0,1:T(1,128)} %copy-done.6) | copy-start | bytes 242692
  323.7 5.2 %collective-permute-start.29 = (f32[15,256]{1,0:T(8,128)S(1)}, f32[15,256]{1,0:T(8,128)S(1)}, u32[]{:S(2)}, u32[]{:S(2)}) collective-permute-start(f32[15,256]{1,0:T(8,128)S(1)} %bitcast.708), channel_id=1, source_target_pairs={{16,0},{32,16},{48,32},{64,48},{80,64},{96,80},{112,96},{17,1},{33... | collective-permute-start | bytes 46088 | tf_op jit(solution)/shard_map/ppermute | solution.py:23
  325.0 4.7 %collective-permute-start.28 = (f32[15,256]{1,0:T(8,128)S(1)}, f32[15,256]{1,0:T(8,128)S(1)}, u32[]{:S(2)}, u32[]{:S(2)}) collective-permute-start(f32[15,256]{1,0:T(8,128)S(1)} %bitcast.704), channel_id=1, source_target_pairs={{0,16},{16,32},{32,48},{48,64},{64,80},{80,96},{96,112},{1,17},{17... | collective-permute-start | bytes 46088 | tf_op jit(solution)/shard_map/ppermute | solution.py:22
  329.7 6.1 %collective-permute-start.31 = (f32[94,15]{1,0:T(8,128)S(1)}, f32[94,15]{1,0:T(8,128)S(1)}, u32[]{:S(2)}, u32[]{:S(2)}) collective-permute-start(f32[94,15]{1,0:T(8,128)S(1)} %get-tuple-element.99), channel_id=1, source_target_pairs={{1,0},{2,1},{3,2},{4,3},{5,4},{6,5},{7,6},{8,7},{9,8},{10,9},{11,1... | collective-permute-start | bytes 16928 | tf_op jit(solution)/shard_map/ppermute | solution.py:23
  333.4 6.0 %collective-permute-start.30 = (f32[94,15]{1,0:T(8,128)S(1)}, f32[94,15]{1,0:T(8,128)S(1)}, u32[]{:S(2)}, u32[]{:S(2)}) collective-permute-start(f32[94,15]{1,0:T(8,128)S(1)} %get-tuple-element.100), channel_id=1, source_target_pairs={{0,1},{1,2},{2,3},{3,4},{4,5},{5,6},{6,7},{7,8},{8,9},{9,10},{10,1... | collective-permute-start | bytes 16928 | tf_op jit(solution)/shard_map/ppermute | solution.py:22
  344.7 60.8 %copy-start.46 = (f32[64,256]{1,0:T(8,128)S(1)}, f32[64,256]{1,0:T(8,128)}, u32[]{:S(2)}) copy-start(f32[64,256]{1,0:T(8,128)} %param.4) | copy-start | bytes 196612
  344.7 60.8 %copy-start.48 = (f32[64,256]{1,0:T(8,128)S(1)}, f32[64,256]{1,0:T(8,128)}, u32[]{:S(2)}) copy-start(f32[64,256]{1,0:T(8,128)} %copy-done.47) | copy-start | bytes 196612
  344.8 60.8 %copy-start.49 = (f32[64,256]{1,0:T(8,128)S(1)}, f32[64,256]{1,0:T(8,128)}, u32[]{:S(2)}) copy-start(f32[64,256]{1,0:T(8,128)} %get-tuple-element.33) | copy-start | bytes 196612
  (28 other events, 318.1 us)
